TPU v7x, 32 devices: a whole 2x2x4 slice. The times are simulated.
32 devices in a mesh: batch: 2 (over core), expert: 16 (over z, y, x).
Axes of the slice: x: 2, y: 2, z: 4, core: 2. Of those that a mesh axis runs over, the one named last changes fastest.
Arguments:
- section_inputs: bfloat16 [4, 4096, 2048], P(None, ('batch', 'expert')), may hold values from -6 to 6
- adjoint_end: bfloat16 [4096, 2048], P(('batch', 'expert')), may hold values from -6 to 6
- gate_probs: float32 [4, 4096, 2], P(None, ('batch', 'expert')), may hold values from 0.2 to 1
- expert_ids: int32 [4, 4096, 2], P(None, ('batch', 'expert')), may hold values from 0 to 15, all different within a row
- norm_gain: float32 [2048], replicated, may hold values from 0.1 to 1.9
- gate_weight: bfloat16 [16, 2048, 384], P('expert'), may hold values from -0.125 to 0.125
- up_weight: bfloat16 [16, 2048, 384], P('expert'), may hold values from -0.125 to 0.125
- down_weight: bfloat16 [16, 2048, 384], P('expert'), may hold values from -0.3125 to 0.3125
Outputs:
- adjoint_start: float32 [4096, 2048], P(('batch', 'expert'))
- gate_grad: float32 [16, 2048, 384], P('expert', 'batch')
- up_grad: float32 [16, 2048, 384], P('expert', 'batch')
- down_grad: float32 [16, 2048, 384], P('expert', 'batch')
Inputs may be any that keep to these rules, and one draw needn't show every extreme that they name: `expert_ids`: the 2 experts of a token in a section differ.
All inputs are finite; a program needn't handle non-finite values.
Results may differ from a plain program's by a relative error of at most 0.0095.
Values may be sent and summed in bfloat16 or wider, within the bound.
No kernel may reach another device: no remote copies, remote signals or barrier semaphores. Data moves between devices by JAX's collectives and lax.ppermute only.
A program may use at most 128 MiB of HBM per device.

v0:
```python
import jax
import jax.numpy as jnp
from jax import lax
from jax.sharding import PartitionSpec as P

SECTIONS = 4
TOP = 2


EPS = 1e-06
STEP = 1.0
ALONG_END = (1.0 / 6.0, 1.0 / 3.0, 1.0 / 3.0, 1.0 / 6.0)
ALONG_NEXT = (0.5, 0.5, 1.0, 0.0)


def contract_rows(left_op, right_op):
    return lax.dot_general(
        left_op, right_op, (((0,), (0,)), ((), ())), preferred_element_type=jnp.float32
    )


def contract_cols(left_op, right_op):
    return lax.dot_general(
        left_op, right_op, (((1,), (1,)), ((), ())), preferred_element_type=jnp.float32
    )


def normalize(inputs, gain_row):
    values = inputs.astype(jnp.float32)
    inverse = lax.rsqrt(jnp.mean(values * values, axis=-1, keepdims=True) + EPS)
    return ((values * inverse * gain_row).astype(jnp.bfloat16), values, inverse)


def norm_back(values, inverse, gain_row, cotangent):
    weighted = gain_row * cotangent
    return inverse * weighted - values * (inverse * inverse * inverse) * jnp.mean(
        values * weighted, axis=-1, keepdims=True
    )


def expert_back(rows_in, rows_cot, gate_mat, up_mat, down_mat):
    gate_pre = jnp.dot(rows_in, gate_mat, preferred_element_type=jnp.float32)
    upward = jnp.dot(rows_in, up_mat, preferred_element_type=jnp.float32)
    logistic = jax.nn.sigmoid(gate_pre)
    active = gate_pre * logistic
    hidden = (active * upward).astype(jnp.bfloat16)
    grad_hidden = jnp.dot(rows_cot, down_mat, preferred_element_type=jnp.float32)
    grad_gate = (grad_hidden * upward * (logistic * (1.0 + gate_pre * (1.0 - logistic)))).astype(
        jnp.bfloat16
    )
    grad_up = (grad_hidden * active).astype(jnp.bfloat16)
    rows_back = (contract_cols(grad_gate, gate_mat) + contract_cols(grad_up, up_mat)).astype(
        jnp.bfloat16
    )
    return (rows_back, hidden, grad_gate, grad_up)


def route(chosen, experts, capacity):
    flat_ids = chosen.reshape(-1)
    hit_table = (flat_ids[:, None] == jnp.arange(experts, dtype=jnp.int32)[None, :]).astype(
        jnp.int32
    )
    before = jnp.cumsum(hit_table, axis=0) - hit_table
    slot_index = jnp.sum(before * hit_table, axis=1)
    is_kept = slot_index < capacity
    target = jnp.where(is_kept, flat_ids * capacity + slot_index, experts * capacity)
    places = jnp.arange(experts * capacity, dtype=jnp.int32)
    match_table = (places[:, None] == target[None, :]).astype(jnp.int32)
    owner_row = jnp.sum(
        match_table * jnp.arange(flat_ids.shape[0], dtype=jnp.int32)[None, :], axis=1
    )
    filled = jnp.sum(match_table, axis=1) > 0
    return (target, is_kept, owner_row, filled)


def pack(source_rows, row_index, filled):
    return jnp.where(filled[:, None], source_rows[row_index], jnp.zeros((), source_rows.dtype))


def on_device(
    section_inputs,
    adjoint_end,
    gate_probs,
    expert_ids,
    norm_gain,
    gate_weight,
    up_weight,
    down_weight,
):
    experts = lax.axis_size("expert")
    tokens = adjoint_end.shape[0]
    model_width = adjoint_end.shape[1]
    capacity = max(2, TOP * tokens // experts)
    end_adjoint = adjoint_end.astype(jnp.float32)
    gate_mat = gate_weight[0]
    up_mat = up_weight[0]
    down_mat = down_weight[0]
    routes = [route(expert_ids[number], experts, capacity) for number in range(SECTIONS)]
    normal = [normalize(section_inputs[number], norm_gain) for number in range(SECTIONS)]
    kept_in = []
    kept_cot = []
    kept_hidden = []
    kept_gate = []
    kept_up = []
    adjoint_start = end_adjoint
    following = jnp.zeros_like(end_adjoint)
    for number in (3, 2, 1, 0):
        target, is_kept, owner_row, filled = routes[number]
        normed, values, inverse = normal[number]
        cotangent = STEP * ALONG_END[number] * end_adjoint + STEP * ALONG_NEXT[number] * following
        rows_cot = (
            (gate_probs[number][:, :, None] * cotangent[:, None, :])
            .astype(jnp.bfloat16)
            .reshape(tokens * TOP, model_width)
        )
        sent_cot = pack(rows_cot, owner_row, filled)
        held_in, held_cot = (
            lax.all_to_all(
                pack(normed, owner_row // TOP, filled),
                "expert",
                split_axis=0,
                concat_axis=0,
                tiled=True,
            ),
            lax.all_to_all(sent_cot, "expert", split_axis=0, concat_axis=0, tiled=True),
        )
        rows_back, hidden, grad_gate, grad_up = expert_back(
            held_in, held_cot, gate_mat, up_mat, down_mat
        )
        kept_in.append(held_in)
        kept_cot.append(held_cot)
        kept_hidden.append(hidden)
        kept_gate.append(grad_gate)
        kept_up.append(grad_up)
        returned = lax.all_to_all(rows_back, "expert", split_axis=0, concat_axis=0, tiled=True)
        picked = jnp.where(
            is_kept[:, None],
            returned[jnp.minimum(target, returned.shape[0] - 1)],
            jnp.zeros((), returned.dtype),
        ).astype(jnp.float32)
        grad_in = picked.reshape(tokens, TOP, model_width).sum(axis=1)
        following = norm_back(values, inverse, norm_gain, grad_in)
        adjoint_start = adjoint_start + following
    every_in = jnp.concatenate(kept_in, axis=0)
    every_cot = jnp.concatenate(kept_cot, axis=0)
    total_gate = contract_rows(every_in, jnp.concatenate(kept_gate, axis=0))
    total_up = contract_rows(every_in, jnp.concatenate(kept_up, axis=0))
    total_down = contract_rows(every_cot, jnp.concatenate(kept_hidden, axis=0))
    summed = (
        lax.psum_scatter(
            total_gate.astype(jnp.bfloat16), "batch", scatter_dimension=0, tiled=True
        ).astype(jnp.float32),
        lax.psum_scatter(
            total_up.astype(jnp.bfloat16), "batch", scatter_dimension=0, tiled=True
        ).astype(jnp.float32),
        lax.psum_scatter(
            total_down.astype(jnp.bfloat16), "batch", scatter_dimension=0, tiled=True
        ).astype(jnp.float32),
    )
    return (adjoint_start, summed[0][None], summed[1][None], summed[2][None])


def solution(mesh):
    in_specs = (
        P(None, ("batch", "expert"), None),
        P(("batch", "expert"), None),
        P(None, ("batch", "expert"), None),
        P(None, ("batch", "expert"), None),
        P(),
        P("expert", None, None),
        P("expert", None, None),
        P("expert", None, None),
    )
    out_specs = (
        P(("batch", "expert"), None),
        P("expert", "batch", None),
        P("expert", "batch", None),
        P("expert", "batch", None),
    )
    return jax.shard_map(
        on_device, mesh=mesh, in_specs=in_specs, out_specs=out_specs, check_vma=False
    )
```

profile of v0, /device:TPU:8, one launch (start us, length us, event | category | flops | bytes accessed | tf_op | source)
XLA Modules:
  0.0 525.3 jit_solution(13199054182619030903)
XLA Ops:
  12.9 2.5 mul.556
  15.4 3.7 mul.557
  22.7 2.3 gather_fusion
  26.3 2.3 gather_fusion.1
  28.7 2.4 broadcast_select_fusion.11
  31.1 33.0 %all_to_all.120 = bf16[16,16,2048]{2,1,0:T(8,128)(2,1)} all-to-all(bf16[16,16,2048]{2,1,0:T(8,128)(2,1)S(1)} %get-tuple-element.55), channel_id=1, replica_groups=mesh['batch'=2,'expert'=16] {'expert'}, dimensions={0} | all-to-all | bytes 2097152 | tf_op jit(solution)/shard_map/all_to_all | solution.py:118
  64.0 4.8 all-to-all-start
  70.5 1.9 fusion.29
  72.5 21.0 %all-to-all-done = bf16[16,16,2048]{2,1,0:T(8,128)(2,1)} async-done(((bf16[16,16,2048]{2,1,0:T(8,128)(2,1)}), bf16[16,16,2048]{2,1,0:T(8,128)(2,1)}, u32[]{:S(2)}, u32[]{:S(2)}) %all-to-all-start) | async-done | bytes 1048608 | tf_op jit(solution)/shard_map/all_to_all | solution.py:125
  93.5 2.5 fusion.49
  100.0 5.2 all-to-all-start.2
  107.6 21.7 %all-to-all-done.2 = bf16[16,16,2048]{2,1,0:T(8,128)(2,1)S(1)} async-done(((bf16[16,16,2048]{2,1,0:T(8,128)(2,1)}), bf16[16,16,2048]{2,1,0:T(8,128)(2,1)S(1)}, u32[]{:S(2)}, u32[]{:S(2)}) %all-to-all-start.2) | async-done | bytes 1048608 | tf_op jit(solution)/shard_map/all_to_all | solution.py:135
  129.3 2.3 gather_fusion.2
  133.4 3.9 convert_reduce_fusion.3
  138.9 2.5 mul.587
  141.4 3.7 mul.588
  146.8 2.3 gather_fusion.3
  149.2 2.3 gather_fusion.4
  151.5 2.4 broadcast_select_fusion.9
  153.9 29.1 %all_to_all.121 = bf16[16,16,2048]{2,1,0:T(8,128)(2,1)} all-to-all(bf16[16,16,2048]{2,1,0:T(8,128)(2,1)S(1)} %get-tuple-element.53), channel_id=1, replica_groups=mesh['batch'=2,'expert'=16] {'expert'}, dimensions={0} | all-to-all | bytes 2097152 | tf_op jit(solution)/shard_map/all_to_all | solution.py:118
  183.0 4.8 all-to-all-start.3
  189.7 1.9 fusion.25
  191.6 20.1 %all-to-all-done.3 = bf16[16,16,2048]{2,1,0:T(8,128)(2,1)} async-done(((bf16[16,16,2048]{2,1,0:T(8,128)(2,1)}), bf16[16,16,2048]{2,1,0:T(8,128)(2,1)}, u32[]{:S(2)}, u32[]{:S(2)}) %all-to-all-start.3) | async-done | bytes 1048608 | tf_op jit(solution)/shard_map/all_to_all | solution.py:125
  211.7 2.5 fusion.47
  218.2 5.6 %all-to-all-start.5 = ((bf16[16,16,2048]{2,1,0:T(8,128)(2,1)}), bf16[16,16,2048]{2,1,0:T(8,128)(2,1)S(1)}, u32[]{:S(2)}, u32[]{:S(2)}) async-start(bf16[16,16,2048]{2,1,0:T(8,128)(2,1)} %bitcast.258), calls=%async_computation.5 | async-start | bytes 2097152 | tf_op jit(solution)/shard_map/all_to_all | solution.py:135
  226.2 21.7 %all-to-all-done.5 = bf16[16,16,2048]{2,1,0:T(8,128)(2,1)S(1)} async-done(((bf16[16,16,2048]{2,1,0:T(8,128)(2,1)}), bf16[16,16,2048]{2,1,0:T(8,128)(2,1)S(1)}, u32[]{:S(2)}, u32[]{:S(2)}) %all-to-all-start.5) | async-done | bytes 1048608 | tf_op jit(solution)/shard_map/all_to_all | solution.py:135
  247.9 2.3 gather_fusion.5
  252.0 3.9 convert_reduce_fusion.2
  257.4 2.5 mul.618
  259.9 3.7 mul.619
  265.4 2.3 gather_fusion.6
  267.7 2.3 gather_fusion.7
  270.0 2.4 broadcast_select_fusion.7
  272.4 29.1 %all_to_all.122 = bf16[16,16,2048]{2,1,0:T(8,128)(2,1)} all-to-all(bf16[16,16,2048]{2,1,0:T(8,128)(2,1)S(1)} %get-tuple-element.51), channel_id=1, replica_groups=mesh['batch'=2,'expert'=16] {'expert'}, dimensions={0} | all-to-all | bytes 2097152 | tf_op jit(solution)/shard_map/all_to_all | solution.py:118
  301.6 5.2 all-to-all-start.6
  308.5 1.9 fusion.21
  310.4 20.0 %all-to-all-done.6 = bf16[16,16,2048]{2,1,0:T(8,128)(2,1)} async-done(((bf16[16,16,2048]{2,1,0:T(8,128)(2,1)}), bf16[16,16,2048]{2,1,0:T(8,128)(2,1)}, u32[]{:S(2)}, u32[]{:S(2)}) %all-to-all-start.6) | async-done | bytes 1048608 | tf_op jit(solution)/shard_map/all_to_all | solution.py:125
  330.4 2.5 fusion.45
  336.9 5.0 all-to-all-start.8
  344.4 21.7 %all-to-all-done.8 = bf16[16,16,2048]{2,1,0:T(8,128)(2,1)S(1)} async-done(((bf16[16,16,2048]{2,1,0:T(8,128)(2,1)}), bf16[16,16,2048]{2,1,0:T(8,128)(2,1)S(1)}, u32[]{:S(2)}, u32[]{:S(2)}) %all-to-all-start.8) | async-done | bytes 1048608 | tf_op jit(solution)/shard_map/all_to_all | solution.py:135
  366.1 2.3 gather_fusion.8
  370.2 3.9 convert_reduce_fusion.1
  375.6 2.5 mul.649
  378.2 3.7 mul.650
  383.6 2.3 gather_fusion.9
  385.9 2.3 gather_fusion.10
  388.3 2.4 broadcast_select_fusion.5
  390.7 29.1 %all_to_all.123 = bf16[16,16,2048]{2,1,0:T(8,128)(2,1)} all-to-all(bf16[16,16,2048]{2,1,0:T(8,128)(2,1)S(1)} %get-tuple-element.49), channel_id=1, replica_groups=mesh['batch'=2,'expert'=16] {'expert'}, dimensions={0} | all-to-all | bytes 2097152 | tf_op jit(solution)/shard_map/all_to_all | solution.py:118
  419.8 4.8 all-to-all-start.9
  424.9 1.9 fusion.17
  426.9 21.6 %all-to-all-done.9 = bf16[16,16,2048]{2,1,0:T(8,128)(2,1)} async-done(((bf16[16,16,2048]{2,1,0:T(8,128)(2,1)}), bf16[16,16,2048]{2,1,0:T(8,128)(2,1)}, u32[]{:S(2)}, u32[]{:S(2)}) %all-to-all-start.9) | async-done | bytes 1048608 | tf_op jit(solution)/shard_map/all_to_all | solution.py:125
  448.5 2.5 fusion.43
  452.6 5.8 %fusion.8 = bf16[2048,384]{1,0:T(8,128)(2,1)} fusion(bf16[256,2048]{1,0:T(8,128)(2,1)} %bitcast.50, bf16[256,2048]{1,0:T(8,128)(2,1)} %bitcast.36, bf16[256,2048]{1,0:T(8,128)(2,1)} %bitcast.22, bf16[256,2048]{1,0:T(8,128)(2,1)} %bitcast.5, bf16[256,384]{1,0:T(8,128)(2,1)S(1)} %get-tuple-element.33, bf16[256,384]{1,0:T(8,128)(2,1)S(1)} %copy-done.82, ...), kind=kOutput, calls=%fused_computation.21 | convolution fusion | flops 1631322112 | bytes 6553600 | tf_op jit(solution)/shard_map/dot_general | solution.py:17
  458.5 5.8 %convolution_convert_fusion = bf16[2048,384]{1,0:T(8,128)(2,1)} fusion(bf16[256,384]{1,0:T(8,128)(2,1)} %get-tuple-element.35, bf16[256,384]{1,0:T(8,128)(2,1)} %copy-done.31, bf16[256,384]{1,0:T(8,128)(2,1)S(1)} %copy-done.30, bf16[256,384]{1,0:T(8,128)(2,1)S(1)} %copy-done.28, bf16[256,2048]{1,0:T(8,128)(2,1)} %bitcast.253, ...), kind=kOutput, calls=%fused_computation.22 | convolution fusion | flops 1631322112 | bytes 6553600 | tf_op jit(solution)/shard_map/dot_general | solution.py:17
  467.8 5.2 all-to-all-start.11
  473.3 5.7 %convolution_convert_fusion.1 = bf16[2048,384]{1,0:T(8,128)(2,1)} fusion(bf16[256,384]{1,0:T(8,128)(2,1)S(1)} %copy-done.39, bf16[256,384]{1,0:T(8,128)(2,1)S(1)} %copy-done.38, bf16[256,384]{1,0:T(8,128)(2,1)S(1)} %copy-done.36, bf16[256,384]{1,0:T(8,128)(2,1)S(1)} %copy-done.34, bf16[256,2048]{1,0:T(8,128)(2,1)} %bitcast.254, ...), kind=kOutput, calls=%fused_computation.23 | convolution fusion | flops 1631322112 | bytes 6553600 | tf_op jit(solution)/shard_map/dot_general | solution.py:17
  479.5 17.5 %all-to-all-done.11 = bf16[16,16,2048]{2,1,0:T(8,128)(2,1)S(1)} async-done(((bf16[16,16,2048]{2,1,0:T(8,128)(2,1)}), bf16[16,16,2048]{2,1,0:T(8,128)(2,1)S(1)}, u32[]{:S(2)}, u32[]{:S(2)}) %all-to-all-start.11) | async-done | bytes 1048608 | tf_op jit(solution)/shard_map/all_to_all | solution.py:135
  497.0 2.3 gather_fusion.11
  499.3 2.6 gather.83
  502.0 5.3 %convert_reduce_fusion = f32[128,2048]{1,0:T(8,128)S(1)} fusion(bf16[128,2,2048]{2,1,0:T(2,128)(2,1)} %gather.83, pred[128,2]{1,0:T(8,128)(4,1)S(1)} %lt.239), kind=kLoop, calls=%fused_computation.32 | loop fusion | flops 1310720 | bytes 2097408 | tf_op jit(solution)/shard_map/reduce_sum | solution.py:141
  507.7 3.4 fusion.55
  511.2 2.4 bitcast_convert_fusion
  513.5 2.4 bitcast_convert_fusion.1
  515.9 2.4 bitcast_convert_fusion.2
  (309 shorter events, 55.9 us)
Async XLA Ops:
  7.2 88.9 %copy-start = (bf16[1,2048,384]{2,1,0:T(8,128)(2,1)S(1)}, bf16[1,2048,384]{2,1,0:T(8,128)(2,1)}, u32[]{:S(2)}) copy-start(bf16[1,2048,384]{2,1,0:T(8,128)(2,1)} %param.14) | copy-start | bytes 4718596
  9.9 95.3 %copy-start.42 = (s32[256]{0:T(256)}, s32[256]{0:T(256)S(1)}, u32[]{:S(2)}) copy-start(s32[256]{0:T(256)S(1)} %fusion.116) | copy-start | bytes 3076
  20.9 4.2 copy-start.46
  31.1 39.5 %copy-start.1 = (bf16[1,2048,384]{2,1,0:T(8,128)(2,1)S(1)}, bf16[1,2048,384]{2,1,0:T(8,128)(2,1)}, u32[]{:S(2)}) copy-start(bf16[1,2048,384]{2,1,0:T(8,128)(2,1)} %param.13) | copy-start | bytes 4718596
  64.0 29.5 %all-to-all-start = ((bf16[16,16,2048]{2,1,0:T(8,128)(2,1)}), bf16[16,16,2048]{2,1,0:T(8,128)(2,1)}, u32[]{:S(2)}, u32[]{:S(2)}) async-start(bf16[16,16,2048]{2,1,0:T(8,128)(2,1)} %get-tuple-element.54), calls=%async_computation | async-start | bytes 2097152 | tf_op jit(solution)/shard_map/all_to_all | solution.py:125
  100.0 5.4 %copy-start.68 = (f32[1,128,2]{1,2,0:T(2,128)S(1)}, f32[1,128,2]{1,2,0:T(2,128)}, u32[]{:S(2)}) copy-start(f32[1,128,2]{1,2,0:T(2,128)} %get-tuple-element.45) | copy-start | bytes 3076
  100.0 5.6 %copy-start.64 = (s32[2,128]{1,0:T(2,128)S(1)}, s32[2,128]{1,0:T(2,128)}, u32[]{:S(2)}) copy-start(s32[2,128]{1,0:T(2,128)} %eq.167) | copy-start | bytes 3076
  100.0 6.8 %copy-start.61 = (s32[256,1]{0,1:T(1,128)S(1)}, s32[256,1]{0,1:T(1,128)}, u32[]{:S(2)}) copy-start(s32[256,1]{0,1:T(1,128)} %mul.570) | copy-start | bytes 3076
  100.0 29.3 %all-to-all-start.2 = ((bf16[16,16,2048]{2,1,0:T(8,128)(2,1)}), bf16[16,16,2048]{2,1,0:T(8,128)(2,1)S(1)}, u32[]{:S(2)}, u32[]{:S(2)}) async-start(bf16[16,16,2048]{2,1,0:T(8,128)(2,1)} %bitcast.257), calls=%async_computation.2 | async-start | bytes 2097152 | tf_op jit(solution)/shard_map/all_to_all | solution.py:135
  106.6 117.2 %copy-start.41 = (s32[256]{0:T(256)}, s32[256]{0:T(256)S(1)}, u32[]{:S(2)}) copy-start(s32[256]{0:T(256)S(1)} %fusion.113) | copy-start | bytes 3076
  133.4 4.0 copy-start.5
  133.4 4.9 copy-start.14
  133.4 4.9 copy-start.47
  133.4 4.9 copy-start.69
  153.9 34.0 %copy-start.59 = (s32[1,128,2]{1,2,0:T(2,128)S(1)}, s32[1,128,2]{1,2,0:T(2,128)}, u32[]{:S(2)}) copy-start(s32[1,128,2]{1,2,0:T(2,128)} %get-tuple-element.43) | copy-start | bytes 3076
  153.9 34.9 %copy-start.58 = (s32[1,128,2]{1,2,0:T(2,128)S(1)}, s32[1,128,2]{1,2,0:T(2,128)}, u32[]{:S(2)}) copy-start(s32[1,128,2]{1,2,0:T(2,128)} %get-tuple-element.38) | copy-start | bytes 3076
  153.9 35.8 %copy-start.2 = (bf16[1,2048,384]{2,1,0:T(8,128)(2,1)S(1)}, bf16[1,2048,384]{2,1,0:T(8,128)(2,1)}, u32[]{:S(2)}) copy-start(bf16[1,2048,384]{2,1,0:T(8,128)(2,1)} %param.13) | copy-start | bytes 4718596
  183.0 28.7 %all-to-all-start.3 = ((bf16[16,16,2048]{2,1,0:T(8,128)(2,1)}), bf16[16,16,2048]{2,1,0:T(8,128)(2,1)}, u32[]{:S(2)}, u32[]{:S(2)}) async-start(bf16[16,16,2048]{2,1,0:T(8,128)(2,1)} %get-tuple-element.52), calls=%async_computation.3 | async-start | bytes 2097152 | tf_op jit(solution)/shard_map/all_to_all | solution.py:125
  218.2 5.8 %copy-start.67 = (f32[1,128,2]{1,2,0:T(2,128)S(1)}, f32[1,128,2]{1,2,0:T(2,128)}, u32[]{:S(2)}) copy-start(f32[1,128,2]{1,2,0:T(2,128)} %get-tuple-element.47) | copy-start | bytes 3076
  218.2 6.1 %copy-start.65 = (s32[2,128]{1,0:T(2,128)S(1)}, s32[2,128]{1,0:T(2,128)}, u32[]{:S(2)}) copy-start(s32[2,128]{1,0:T(2,128)} %eq.178) | copy-start | bytes 3076
  218.2 7.3 %copy-start.62 = (s32[256,1]{0,1:T(1,128)S(1)}, s32[256,1]{0,1:T(1,128)}, u32[]{:S(2)}) copy-start(s32[256,1]{0,1:T(1,128)} %mul.601) | copy-start | bytes 3076
  218.2 29.7 %all-to-all-start.5 = ((bf16[16,16,2048]{2,1,0:T(8,128)(2,1)}), bf16[16,16,2048]{2,1,0:T(8,128)(2,1)S(1)}, u32[]{:S(2)}, u32[]{:S(2)}) async-start(bf16[16,16,2048]{2,1,0:T(8,128)(2,1)} %bitcast.258), calls=%async_computation.5 | async-start | bytes 2097152 | tf_op jit(solution)/shard_map/all_to_all | solution.py:135
  225.2 116.8 %copy-start.40 = (s32[256]{0:T(256)}, s32[256]{0:T(256)S(1)}, u32[]{:S(2)}) copy-start(s32[256]{0:T(256)S(1)} %fusion.110) | copy-start | bytes 3076
  252.0 4.8 copy-start.15
  252.0 4.8 copy-start.44
  252.0 4.8 copy-start.49
  272.4 34.3 %copy-start.57 = (s32[1,128,2]{1,2,0:T(2,128)S(1)}, s32[1,128,2]{1,2,0:T(2,128)}, u32[]{:S(2)}) copy-start(s32[1,128,2]{1,2,0:T(2,128)} %get-tuple-element.42) | copy-start | bytes 3076
  272.4 35.2 %copy-start.56 = (s32[1,128,2]{1,2,0:T(2,128)S(1)}, s32[1,128,2]{1,2,0:T(2,128)}, u32[]{:S(2)}) copy-start(s32[1,128,2]{1,2,0:T(2,128)} %get-tuple-element.39) | copy-start | bytes 3076
  272.4 36.1 %copy-start.3 = (bf16[1,2048,384]{2,1,0:T(8,128)(2,1)S(1)}, bf16[1,2048,384]{2,1,0:T(8,128)(2,1)}, u32[]{:S(2)}) copy-start(bf16[1,2048,384]{2,1,0:T(8,128)(2,1)} %param.13) | copy-start | bytes 4718596
  301.6 28.9 %all-to-all-start.6 = ((bf16[16,16,2048]{2,1,0:T(8,128)(2,1)}), bf16[16,16,2048]{2,1,0:T(8,128)(2,1)}, u32[]{:S(2)}, u32[]{:S(2)}) async-start(bf16[16,16,2048]{2,1,0:T(8,128)(2,1)} %get-tuple-element.50), calls=%async_computation.6 | async-start | bytes 2097152 | tf_op jit(solution)/shard_map/all_to_all | solution.py:125
  336.9 5.2 copy-start.66
  336.9 5.5 %copy-start.63 = (s32[2,128]{1,0:T(2,128)S(1)}, s32[2,128]{1,0:T(2,128)}, u32[]{:S(2)}) copy-start(s32[2,128]{1,0:T(2,128)} %eq.189) | copy-start | bytes 3076
  336.9 6.7 %copy-start.60 = (s32[256,1]{0,1:T(1,128)S(1)}, s32[256,1]{0,1:T(1,128)}, u32[]{:S(2)}) copy-start(s32[256,1]{0,1:T(1,128)} %mul.632) | copy-start | bytes 3076
  336.9 29.2 %all-to-all-start.8 = ((bf16[16,16,2048]{2,1,0:T(8,128)(2,1)}), bf16[16,16,2048]{2,1,0:T(8,128)(2,1)S(1)}, u32[]{:S(2)}, u32[]{:S(2)}) async-start(bf16[16,16,2048]{2,1,0:T(8,128)(2,1)} %bitcast.256), calls=%async_computation.8 | async-start | bytes 2097152 | tf_op jit(solution)/shard_map/all_to_all | solution.py:135
  370.2 4.8 copy-start.16
  370.2 4.8 copy-start.54
  370.2 4.8 copy-start.71
  390.7 34.2 %copy-start.4 = (bf16[1,2048,384]{2,1,0:T(8,128)(2,1)S(1)}, bf16[1,2048,384]{2,1,0:T(8,128)(2,1)}, u32[]{:S(2)}) copy-start(bf16[1,2048,384]{2,1,0:T(8,128)(2,1)} %param.13) | copy-start | bytes 4718596
  419.8 28.7 %all-to-all-start.9 = ((bf16[16,16,2048]{2,1,0:T(8,128)(2,1)}), bf16[16,16,2048]{2,1,0:T(8,128)(2,1)}, u32[]{:S(2)}, u32[]{:S(2)}) async-start(bf16[16,16,2048]{2,1,0:T(8,128)(2,1)} %get-tuple-element.48), calls=%async_computation.9 | async-start | bytes 2097152 | tf_op jit(solution)/shard_map/all_to_all | solution.py:125
  424.7 86.5 %reduce-scatter.8.cloned.1.call-start = ((), (), s32[]{:S(2)}) async-start(), calls=%async_computation.17 | async-start | bytes 2359296 | tf_op jit(solution)/shard_map/reduce_scatter | solution.py:156
  452.6 5.9 %copy-start.28 = (bf16[256,384]{1,0:T(8,128)(2,1)S(1)}, bf16[256,384]{1,0:T(8,128)(2,1)}, u32[]{:S(2)}) copy-start(bf16[256,384]{1,0:T(8,128)(2,1)} %copy-done.27) | copy-start | bytes 589828
  452.6 5.9 %copy-start.30 = (bf16[256,384]{1,0:T(8,128)(2,1)S(1)}, bf16[256,384]{1,0:T(8,128)(2,1)}, u32[]{:S(2)}) copy-start(bf16[256,384]{1,0:T(8,128)(2,1)} %copy-done.29) | copy-start | bytes 589828
  458.4 55.1 %reduce-scatter.6.cloned.1.call-start = ((), (), s32[]{:S(2)}) async-start(), calls=%async_computation.16 | async-start | bytes 2359296 | tf_op jit(solution)/shard_map/reduce_scatter | solution.py:153
  467.8 5.5 %copy-start.34 = (bf16[256,384]{1,0:T(8,128)(2,1)S(1)}, bf16[256,384]{1,0:T(8,128)(2,1)}, u32[]{:S(2)}) copy-start(bf16[256,384]{1,0:T(8,128)(2,1)} %copy-done.33) | copy-start | bytes 589828
  467.8 5.5 %copy-start.36 = (bf16[256,384]{1,0:T(8,128)(2,1)S(1)}, bf16[256,384]{1,0:T(8,128)(2,1)}, u32[]{:S(2)}) copy-start(bf16[256,384]{1,0:T(8,128)(2,1)} %copy-done.35) | copy-start | bytes 589828
  467.8 5.5 %copy-start.38 = (bf16[256,384]{1,0:T(8,128)(2,1)S(1)}, bf16[256,384]{1,0:T(8,128)(2,1)}, u32[]{:S(2)}) copy-start(bf16[256,384]{1,0:T(8,128)(2,1)} %copy-done.37) | copy-start | bytes 589828
  467.8 5.5 %copy-start.39 = (bf16[256,384]{1,0:T(8,128)(2,1)S(1)}, bf16[256,384]{1,0:T(8,128)(2,1)}, u32[]{:S(2)}) copy-start(bf16[256,384]{1,0:T(8,128)(2,1)} %get-tuple-element.34) | copy-start | bytes 589828
  467.8 29.2 %all-to-all-start.11 = ((bf16[16,16,2048]{2,1,0:T(8,128)(2,1)}), bf16[16,16,2048]{2,1,0:T(8,128)(2,1)S(1)}, u32[]{:S(2)}, u32[]{:S(2)}) async-start(bf16[16,16,2048]{2,1,0:T(8,128)(2,1)} %bitcast.259), calls=%async_computation.11 | async-start | bytes 2097152 | tf_op jit(solution)/shard_map/all_to_all | solution.py:135
  473.0 6.1 %copy-start.55 = (s32[1,128,2]{1,2,0:T(2,128)S(1)}, s32[1,128,2]{1,2,0:T(2,128)}, u32[]{:S(2)}) copy-start(s32[1,128,2]{1,2,0:T(2,128)} %get-tuple-element.36) | copy-start | bytes 3076
  473.0 43.0 %reduce-scatter.4.cloned.1.call-start = ((), (), s32[]{:S(2)}) async-start(), calls=%async_computation.15 | async-start | bytes 2359296 | tf_op jit(solution)/shard_map/reduce_scatter | solution.py:150
  499.3 8.3 %copy-start.12 = (f32[128,2048]{1,0:T(8,128)S(1)}, f32[128,2048]{1,0:T(8,128)}, u32[]{:S(2)}) copy-start(f32[128,2048]{1,0:T(8,128)} %copy-done.11) | copy-start | bytes 3145732
  501.9 5.4 %copy-start.8 = (bf16[4,128,2048]{2,1,0:T(8,128)(2,1)S(1)}, bf16[4,128,2048]{2,1,0:T(8,128)(2,1)}, u32[]{:S(2)}) copy-start(bf16[4,128,2048]{2,1,0:T(8,128)(2,1)} %param.8) | copy-start | bytes 6291460
  501.9 5.7 %copy-start.10 = (f32[128,2048]{1,0:T(8,128)S(1)}, f32[128,2048]{1,0:T(8,128)}, u32[]{:S(2)}) copy-start(f32[128,2048]{1,0:T(8,128)} %copy-done.9) | copy-start | bytes 3145732
  502.0 5.7 %copy-start.17 = (bf16[128,2048]{1,0:T(8,128)(2,1)S(1)}, bf16[128,2048]{1,0:T(8,128)(2,1)}, u32[]{:S(2)}) copy-start(bf16[128,2048]{1,0:T(8,128)(2,1)} %param.9) | copy-start | bytes 1572868
  502.0 5.7 %copy-start.45 = (f32[128]{0:T(128)S(1)}, f32[128]{0:T(128)}, u32[]{:S(2)}) copy-start(f32[128]{0:T(128)} %copy-done.43) | copy-start | bytes 1540
  502.0 5.7 %copy-start.48 = (f32[128]{0:T(128)S(1)}, f32[128]{0:T(128)}, u32[]{:S(2)}) copy-start(f32[128]{0:T(128)} %copy-done.46) | copy-start | bytes 1540
  502.0 5.7 %copy-start.50 = (f32[128]{0:T(128)S(1)}, f32[128]{0:T(128)}, u32[]{:S(2)}) copy-start(f32[128]{0:T(128)} %get-tuple-element.68) | copy-start | bytes 1540
  502.0 5.7 %copy-start.52 = (f32[128]{0:T(128)S(1)}, f32[128]{0:T(128)}, u32[]{:S(2)}) copy-start(f32[128]{0:T(128)} %copy-done.51) | copy-start | bytes 1540
  502.0 5.7 %copy-start.70 = (f32[128]{0:T(128)S(1)}, f32[128]{0:T(128)}, u32[]{:S(2)}) copy-start(f32[128]{0:T(128)} %get-tuple-element.70) | copy-start | bytes 1540
  502.0 5.7 %copy-start.72 = (f32[128]{0:T(128)S(1)}, f32[128]{0:T(128)}, u32[]{:S(2)}) copy-start(f32[128]{0:T(128)} %get-tuple-element.66) | copy-start | bytes 1540
  502.0 5.7 %copy-start.74 = (f32[128]{0:T(128)S(1)}, f32[128]{0:T(128)}, u32[]{:S(2)}) copy-start(f32[128]{0:T(128)} %copy-done.73) | copy-start | bytes 1540
  502.0 5.7 %copy-start.76 = (f32[128]{0:T(128)S(1)}, f32[128]{0:T(128)}, u32[]{:S(2)}) copy-start(f32[128]{0:T(128)} %copy-done.75) | copy-start | bytes 1540
  502.0 5.7 %copy-start.78 = (f32[128]{0:T(128)S(1)}, f32[128]{0:T(128)}, u32[]{:S(2)}) copy-start(f32[128]{0:T(128)} %copy-done.77) | copy-start | bytes 1540
  502.0 5.7 %copy-start.79 = (f32[128]{0:T(128)S(1)}, f32[128]{0:T(128)}, u32[]{:S(2)}) copy-start(f32[128]{0:T(128)} %get-tuple-element.64) | copy-start | bytes 1540
  (30 other events, 53.8 us)
Sparse Core Ops, SparseCore 0:
  458.5 8.2 reduce-scatter.7
  469.7 10.3 reduce-scatter.5
  482.9 10.3 reduce-scatter.3
where the time goes:
time: 534 us; the launch traced here: 525 us
  waiting for transfers between devices  165 us (31%)
  blocking collectives  120 us (22%)
  local copies, waits for them, and re-layouts  70.9 us (13%)
  other arithmetic  60 us (11%)
  matrix products  51.9 us (10%)
  starting transfers between devices  41.2 us (8%)
  between operations  15.5 us (3%)
    all_to_all x4, blocking collectives, on_device(): lax.all_to_all(pack(normed, owner_row // TOP, filled), 'expert', split_ax...  120 us
    all_to_all x4, waiting for transfers between devices, on_device(): lax.all_to_all(sent_cot, 'expert', split_axis=0, concat_axis=0, tiled=True)  82.7 us
    all_to_all x4, waiting for transfers between devices, on_device(): lax.all_to_all(rows_back, 'expert', split_axis=0, concat_axis=0, tiled=True)  82.6 us
    mul x12, local copies, waits for them, and re-layouts, on_device(): gate_probs[number][:, :, None] * cotangent[:, None, :]  25.4 us
    all_to_all x4, starting transfers between devices, on_device(): lax.all_to_all(rows_back, 'expert', split_axis=0, concat_axis=0, tiled=True)  21 us
    all_to_all x4, starting transfers between devices, on_device(): lax.all_to_all(sent_cot, 'expert', split_axis=0, concat_axis=0, tiled=True)  19.6 us
    gather x8, local copies, waits for them, and re-layouts, pack(): source_rows[row_index]  18.6 us
    dot_general x3, matrix products, contract_rows(): lax.dot_general(left_op, right_op, (((0,), (0,)), ((), ())), preferred_el...  17.3 us
  transfers between devices with their start and end apart: 11, of which 8 were waited for; matrix products, arithmetic and copies ran while one was open for 10% of the time, Pallas kernels for 0%

commit v1 on v0

v1 whole, which is shorter than its diff:
```python
import functools

import jax
import jax.numpy as jnp
from jax import lax
from jax.experimental import pallas as pl
from jax.experimental.pallas import tpu as pltpu
from jax.sharding import PartitionSpec as P

SECTIONS = 4
TOP = 2

EPS = 1e-06
STEP = 1.0
ALONG_END = (1.0 / 6.0, 1.0 / 3.0, 1.0 / 3.0, 1.0 / 6.0)
ALONG_NEXT = (0.5, 0.5, 1.0, 0.0)
CHUNK = 256


def contract_rows(left_op, right_op):
    return lax.dot_general(
        left_op, right_op, (((0,), (0,)), ((), ())), preferred_element_type=jnp.float32
    )


def contract_cols(left_op, right_op):
    return lax.dot_general(
        left_op, right_op, (((1,), (1,)), ((), ())), preferred_element_type=jnp.float32
    )


def mxu(left_op, right_op):
    return jnp.dot(left_op, right_op, preferred_element_type=jnp.float32)


def places_of(ids, experts, capacity):
    tokens = ids.shape[1]
    each = lax.broadcasted_iota(jnp.int32, (experts, tokens), 0)
    hits = [each == ids[j : j + 1, :] for j in range(TOP)]
    count = sum(h.astype(jnp.float32) for h in hits).astype(jnp.bfloat16)
    earlier = lax.broadcasted_iota(jnp.int32, (tokens, tokens), 0) < lax.broadcasted_iota(
        jnp.int32, (tokens, tokens), 1
    )
    before = mxu(count, earlier.astype(jnp.float32).astype(jnp.bfloat16))
    place = lax.broadcasted_iota(jnp.int32, (experts * capacity, tokens), 0)
    masks = []
    for j in range(TOP):
        slot = jnp.sum(jnp.where(hits[j], before, 0.0), axis=0, keepdims=True).astype(jnp.int32)
        target = jnp.where(slot < capacity, ids[j : j + 1, :] * capacity + slot, -1)
        masks.append(place == target)
    return masks


def join(masks):
    return sum(m.astype(jnp.float32) for m in masks)


def chunks_of(width):
    return width // CHUNK


def cols(step):
    return pl.ds(pl.multiple_of(step * CHUNK, CHUNK), CHUNK)


def inverse_norm(u_ref):
    tokens, width = u_ref.shape

    def body(step, total):
        part = u_ref[:, cols(step)].astype(jnp.float32)
        return total + jnp.sum(part * part, axis=1, keepdims=True)

    total = lax.fori_loop(0, chunks_of(width), body, jnp.zeros((tokens, 1), jnp.float32))
    return lax.rsqrt(total / width + EPS)


def pack_in_kernel(experts, capacity, ids_ref, u_ref, gain_ref, sent_ref):
    width = u_ref.shape[1]
    pick = join(places_of(ids_ref[...], experts, capacity)).astype(jnp.bfloat16)
    inverse = inverse_norm(u_ref)

    def body(step, _):
        part = u_ref[:, cols(step)].astype(jnp.float32)
        normed = (part * inverse * gain_ref[:, cols(step)]).astype(jnp.bfloat16)
        sent_ref[:, cols(step)] = mxu(pick, normed).astype(jnp.bfloat16)
        return 0

    lax.fori_loop(0, chunks_of(width), body, 0)


def pack_cot(masks, probs, cotangent):
    pick = join(masks).astype(jnp.bfloat16)
    high = cotangent.astype(jnp.bfloat16)
    low = (cotangent - high.astype(jnp.float32)).astype(jnp.bfloat16)
    return (probs * (mxu(pick, high) + mxu(pick, low))).astype(jnp.bfloat16)


def place_probs(masks, probs):
    return sum(
        jnp.sum(jnp.where(masks[j], probs[j : j + 1, :], 0.0), axis=1, keepdims=True)
        for j in range(TOP)
    )


def first_cot_kernel(experts, capacity, along, ids_ref, probs_ref, end_ref, sent_ref):
    width = end_ref.shape[1]
    masks = places_of(ids_ref[...], experts, capacity)
    probs = place_probs(masks, probs_ref[...])

    def body(step, _):
        cotangent = along * end_ref[:, cols(step)].astype(jnp.float32)
        sent_ref[:, cols(step)] = pack_cot(masks, probs, cotangent)
        return 0

    lax.fori_loop(0, chunks_of(width), body, 0)


def combine_kernel(
    experts, capacity, along, ids_ref, next_ids_ref, next_probs_ref, back_ref, u_ref, gain_ref,
    end_ref, total_ref, *out
):
    sent_ref, sum_ref, weighted_ref = out if along else (None, *out)
    tokens, width = u_ref.shape
    pick = join(places_of(ids_ref[...], experts, capacity)).T.astype(jnp.bfloat16)

    def first(step, carry):
        square, cross = carry
        part = u_ref[:, cols(step)].astype(jnp.float32)
        weighted = gain_ref[:, cols(step)] * mxu(pick, back_ref[:, cols(step)])
        weighted_ref[:, cols(step)] = weighted
        return (
            square + jnp.sum(part * part, axis=1, keepdims=True),
            cross + jnp.sum(part * weighted, axis=1, keepdims=True),
        )

    zero = jnp.zeros((tokens, 1), jnp.float32)
    square, cross = lax.fori_loop(0, chunks_of(width), first, (zero, zero))
    inverse = lax.rsqrt(square / width + EPS)
    scale = inverse * inverse * inverse * (cross / width)
    if along:
        masks = places_of(next_ids_ref[...], experts, capacity)
        probs = place_probs(masks, next_probs_ref[...])

    def second(step, _):
        part = u_ref[:, cols(step)].astype(jnp.float32)
        following = inverse * weighted_ref[:, cols(step)] - part * scale
        sum_ref[:, cols(step)] = total_ref[:, cols(step)].astype(jnp.float32) + following
        if along:
            end = end_ref[:, cols(step)].astype(jnp.float32)
            sent_ref[:, cols(step)] = pack_cot(
                masks, probs, along[0] * end + along[1] * following
            )
        return 0

    lax.fori_loop(0, chunks_of(width), second, 0)


def call(kernel, outs, scratch=(), flops=0, moved=0):
    return pl.pallas_call(
        kernel,
        out_shape=outs,
        scratch_shapes=list(scratch),
        cost_estimate=pl.CostEstimate(flops=flops, bytes_accessed=moved, transcendentals=0),
        compiler_params=pltpu.CompilerParams(vmem_limit_bytes=24 * 2**20),
    )


def expert_front(rows_in, gate_mat, up_mat):
    gate_pre = mxu(rows_in, gate_mat)
    upward = mxu(rows_in, up_mat)
    logistic = jax.nn.sigmoid(gate_pre)
    active = gate_pre * logistic
    hidden = (active * upward).astype(jnp.bfloat16)
    slope = upward * (logistic * (1.0 + gate_pre * (1.0 - logistic)))
    return (slope, active, hidden)


def expert_back(rows_cot, slope, active, gate_mat, up_mat, down_mat):
    grad_hidden = mxu(rows_cot, down_mat)
    grad_gate = (grad_hidden * slope).astype(jnp.bfloat16)
    grad_up = (grad_hidden * active).astype(jnp.bfloat16)
    rows_back = (contract_cols(grad_gate, gate_mat) + contract_cols(grad_up, up_mat)).astype(
        jnp.bfloat16
    )
    return (rows_back, grad_gate, grad_up)


def exchange(rows):
    return lax.all_to_all(rows, "expert", split_axis=0, concat_axis=0, tiled=True)


def on_device(
    section_inputs,
    adjoint_end,
    gate_probs,
    expert_ids,
    norm_gain,
    gate_weight,
    up_weight,
    down_weight,
):
    experts = lax.axis_size("expert")
    tokens, width = adjoint_end.shape
    capacity = max(2, TOP * tokens // experts)
    places = experts * capacity
    gate_mat = gate_weight[0]
    up_mat = up_weight[0]
    down_mat = down_weight[0]
    gain = norm_gain.reshape(1, width)
    ids = jnp.transpose(expert_ids, (0, 2, 1))
    probs = jnp.transpose(gate_probs, (0, 2, 1))
    rows = jax.ShapeDtypeStruct((places, width), jnp.bfloat16)
    wide = jax.ShapeDtypeStruct((tokens, width), jnp.float32)
    work = 2 * places * tokens * width

    held_in = {}
    for number in (3, 2, 1, 0):
        sent_in = call(
            functools.partial(pack_in_kernel, experts, capacity), rows, flops=work, moved=3 * 2**19
        )(ids[number], section_inputs[number], gain)
        held_in[number] = exchange(sent_in)
    sent_cot = call(
        functools.partial(first_cot_kernel, experts, capacity, STEP * ALONG_END[3]),
        rows,
        flops=2 * work,
        moved=3 * 2**19,
    )(ids[3], probs[3], adjoint_end)
    kept = []
    total = adjoint_end
    for number in (3, 2, 1, 0):
        slope, active, hidden = expert_front(held_in[number], gate_mat, up_mat)
        held_cot = exchange(sent_cot)
        rows_back, grad_gate, grad_up = expert_back(
            held_cot, slope, active, gate_mat, up_mat, down_mat
        )
        kept.append((held_in[number], held_cot, hidden, grad_gate, grad_up))
        returned = exchange(rows_back)
        following = max(number - 1, 0)
        along = (
            (STEP * ALONG_END[following], STEP * ALONG_NEXT[following]) if number else None
        )
        results = call(
            functools.partial(combine_kernel, experts, capacity, along),
            (rows, wide) if number else (wide,),
            scratch=[pltpu.VMEM((tokens, width), jnp.float32)],
            flops=3 * work,
            moved=6 * 2**20,
        )(
            ids[number], ids[following], probs[following], returned, section_inputs[number],
            gain, adjoint_end, total
        )
        if number:
            sent_cot, total = results
        else:
            (total,) = results
    every_in, every_cot, every_hidden, every_gate, every_up = (
        jnp.concatenate(parts, axis=0) for parts in zip(*kept)
    )
    pairs = ((every_in, every_gate), (every_in, every_up), (every_cot, every_hidden))
    halves = lax.axis_size("batch")
    if halves != 2:
        summed = [
            lax.psum_scatter(contract_rows(*pair), "batch", scatter_dimension=0, tiled=True)
            for pair in pairs
        ]
    else:
        mine = lax.axis_index("batch")
        half = width // halves

        def part(pair, which):
            return contract_rows(
                lax.dynamic_slice_in_dim(pair[0], which * half, half, axis=1), pair[1]
            )

        others = [part(pair, 1 - mine).astype(jnp.bfloat16) for pair in pairs]
        came = [lax.ppermute(other, "batch", [(0, 1), (1, 0)]) for other in others]
        summed = [part(pair, mine) + one.astype(jnp.float32) for pair, one in zip(pairs, came)]
    return (total, summed[0][None], summed[1][None], summed[2][None])


def solution(mesh):
    in_specs = (
        P(None, ("batch", "expert"), None),
        P(("batch", "expert"), None),
        P(None, ("batch", "expert"), None),
        P(None, ("batch", "expert"), None),
        P(),
        P("expert", None, None),
        P("expert", None, None),
        P("expert", None, None),
    )
    out_specs = (
        P(("batch", "expert"), None),
        P("expert", "batch", None),
        P("expert", "batch", None),
        P("expert", "batch", None),
    )
    return jax.shard_map(
        on_device, mesh=mesh, in_specs=in_specs, out_specs=out_specs, check_vma=False
    )
```

time: 534 us -> 408 us (0.76); the launches traced: 525 us -> 406 us
  blocking collectives: 120 us -> 0 us
  waiting for transfers between devices: 165 us -> 222 us
  other arithmetic: 60 us -> 5 us
  local copies, waits for them, and re-layouts: 70.9 us -> 22 us
  Pallas kernels: 0 us -> 34.2 us
  starting transfers between devices: 41.2 us -> 61 us
  between operations: 15.5 us -> 1.28 us
  matrix products: 51.9 us -> 61 us
    all_to_all x4 -> x0, blocking collectives: 120 us -> none  [on_device(): lax.all_to_all(pack(normed, owner_row // TOP, filled), 'expert', split_ax...]
    all_to_all x8 -> x12, waiting for transfers between devices: 165 us -> 222 us  [exchange(): lax.all_to_all(rows, 'expert', split_axis=0, concat_axis=0, tiled=True)]
    gather x16 -> x0, local copies, waits for them, and re-layouts: 35.8 us -> none  [the longest x8 18.6 us: pack(): source_rows[row_index]]
    pallas_call x0 -> x9, Pallas kernels: none -> 34.2 us  [the longest x4 22.5 us: on_device(): call(functools.partial(combine_kernel, experts, capacity, along), (rows,...]
    mul x20 -> x0, local copies, waits for them, and re-layouts: 28.1 us -> none  [the longest x12 25.4 us: on_device(): gate_probs[number][:, :, None] * cotangent[:, None, :]]
    reduce_sum x17 -> x0, other arithmetic: 20.5 us -> none  [the longest x4 17 us: on_device(): grad_in = picked.reshape(tokens, TOP, model_width).sum(axis=1)]
    all_to_all x8 -> x12, starting transfers between devices: 40.7 us -> 60.5 us  [exchange(): lax.all_to_all(rows, 'expert', split_axis=0, concat_axis=0, tiled=True)]
    unnamed x166 -> x112, local copies, waits for them, and re-layouts: 0.37 us -> 18.5 us
  transfers between devices with their start and end apart: 11 -> 15, of which waited for: 8 -> 12; matrix products, arithmetic and copies ran while one was open for 10% -> 8% of each run, Pallas kernels for 0% -> 7%
where the time goes in v1:
time: 408 us; the launch traced here: 406 us
  waiting for transfers between devices  222 us (54%)
  starting transfers between devices  61 us (15%)
  matrix products  61 us (15%)
  Pallas kernels  34.2 us (8%)
  local copies, waits for them, and re-layouts  22 us (5%)
  other arithmetic  5 us (1%)
    all_to_all x12, waiting for transfers between devices, exchange(): lax.all_to_all(rows, 'expert', split_axis=0, concat_axis=0, tiled=True)  222 us
    all_to_all x12, starting transfers between devices, exchange(): lax.all_to_all(rows, 'expert', split_axis=0, concat_axis=0, tiled=True)  60.5 us
    dot_general x12, matrix products, mxu(): return jnp.dot(left_op, right_op, preferred_element_type=jnp.float32)  32.7 us
    pallas_call x4, Pallas kernels, on_device(): call(functools.partial(combine_kernel, experts, capacity, along), (rows,...  22.5 us
    unnamed x112, local copies, waits for them, and re-layouts  18.5 us
    dot_general x6, matrix products, contract_rows(): lax.dot_general(left_op, right_op, (((0,), (0,)), ((), ())), preferred_el...  18.5 us
    dot_general x8, matrix products, contract_cols(): lax.dot_general(left_op, right_op, (((1,), (1,)), ((), ())), preferred_el...  9.93 us
    pallas_call x4, Pallas kernels, on_device(): call(functools.partial(pack_in_kernel, experts, capacity), rows, flops=wo...  9.48 us
  transfers between devices with their start and end apart: 15, of which 12 were waited for; matrix products, arithmetic and copies ran while one was open for 8% of the time, Pallas kernels for 7%

profile of v1, /device:TPU:8, one launch (start us, length us, event | category | flops | bytes accessed | tf_op | source)
XLA Modules:
  0.0 406.1 jit_solution(2887393189549601411)
XLA Ops:
  1.5 2.6 slice_bitcast_fusion
  4.1 2.4 shard_map.112
  8.2 7.2 %all-to-all-start.1 = ((bf16[16,16,2048]{2,1,0:T(8,128)(2,1)}), bf16[16,16,2048]{2,1,0:T(8,128)(2,1)}, u32[]{:S(2)}, u32[]{:S(2)}) async-start(bf16[16,16,2048]{2,1,0:T(8,128)(2,1)} %bitcast.131), calls=%async_computation.1 | async-start | bytes 2097152 | tf_op jit(solution)/shard_map/all_to_all | solution.py:189
  15.5 2.2 shard_map.111
  18.6 22.4 %all-to-all-done.1 = bf16[16,16,2048]{2,1,0:T(8,128)(2,1)} async-done(((bf16[16,16,2048]{2,1,0:T(8,128)(2,1)}), bf16[16,16,2048]{2,1,0:T(8,128)(2,1)}, u32[]{:S(2)}, u32[]{:S(2)}) %all-to-all-start.1) | async-done | bytes 1048608 | tf_op jit(solution)/shard_map/all_to_all | solution.py:189
  41.1 4.7 %all-to-all-start = ((bf16[16,16,2048]{2,1,0:T(8,128)(2,1)}), bf16[16,16,2048]{2,1,0:T(8,128)(2,1)}, u32[]{:S(2)}, u32[]{:S(2)}) async-start(bf16[16,16,2048]{2,1,0:T(8,128)(2,1)} %bitcast.132), calls=%async_computation | async-start | bytes 2097152 | tf_op jit(solution)/shard_map/all_to_all | solution.py:189
  45.8 3.2 fusion.30
  49.0 21.0 %all-to-all-done = bf16[16,16,2048]{2,1,0:T(8,128)(2,1)} async-done(((bf16[16,16,2048]{2,1,0:T(8,128)(2,1)}), bf16[16,16,2048]{2,1,0:T(8,128)(2,1)}, u32[]{:S(2)}, u32[]{:S(2)}) %all-to-all-start) | async-done | bytes 1048608 | tf_op jit(solution)/shard_map/all_to_all | solution.py:189
  70.1 2.5 fusion.50
  72.6 2.8 multiply_convert_fusion.3
  76.2 1.8 fusion
  77.9 4.9 %all-to-all-start.2 = ((bf16[16,16,2048]{2,1,0:T(8,128)(2,1)}), bf16[16,16,2048]{2,1,0:T(8,128)(2,1)}, u32[]{:S(2)}, u32[]{:S(2)}) async-start(bf16[16,16,2048]{2,1,0:T(8,128)(2,1)} %bitcast.146), calls=%async_computation.2 | async-start | bytes 2097152 | tf_op jit(solution)/shard_map/all_to_all | solution.py:189
  82.8 1.0 copy-done.2
  83.8 2.4 shard_map.114
  87.2 20.0 %all-to-all-done.2 = bf16[16,16,2048]{2,1,0:T(8,128)(2,1)} async-done(((bf16[16,16,2048]{2,1,0:T(8,128)(2,1)}), bf16[16,16,2048]{2,1,0:T(8,128)(2,1)}, u32[]{:S(2)}, u32[]{:S(2)}) %all-to-all-start.2) | async-done | bytes 1048608 | tf_op jit(solution)/shard_map/all_to_all | solution.py:189
  107.2 4.8 %all-to-all-start.4 = ((bf16[16,16,2048]{2,1,0:T(8,128)(2,1)}), bf16[16,16,2048]{2,1,0:T(8,128)(2,1)}, u32[]{:S(2)}, u32[]{:S(2)}) async-start(bf16[16,16,2048]{2,1,0:T(8,128)(2,1)} %bitcast.130), calls=%async_computation.4 | async-start | bytes 2097152 | tf_op jit(solution)/shard_map/all_to_all | solution.py:189
  112.0 1.0 copy-done.5
  113.0 5.9 %shard_map.113 = (bf16[256,2048]{1,0:T(8,128)(2,1)S(1)}, f32[128,2048]{1,0:T(8,128)S(1)}) custom-call(s32[2,128]{1,0:T(2,128)S(1)} %get-tuple-element.36.ids_ref, s32[2,128]{1,0:T(2,128)S(1)} %get-tuple-element.37.next_ids_ref.ids_ref, f32[2,128]{1,0:T(2,128)S(1)} %get-tuple-element.33.next_probs_ref, bf16[256,2048]{1,0:T(8,128)(2,1)} %bitcast.20.back_ref, ...), custom_call_target="tpu_custom_call" | custom-call | flops 402653184 | bytes 6291456 | tf_op jit(solution)/shard_map/pallas_call | solution.py:242
  120.9 15.2 %all-to-all-done.4 = bf16[16,16,2048]{2,1,0:T(8,128)(2,1)} async-done(((bf16[16,16,2048]{2,1,0:T(8,128)(2,1)}), bf16[16,16,2048]{2,1,0:T(8,128)(2,1)}, u32[]{:S(2)}, u32[]{:S(2)}) %all-to-all-start.4) | async-done | bytes 1048608 | tf_op jit(solution)/shard_map/all_to_all | solution.py:189
  136.1 4.9 %all-to-all-start.3 = ((bf16[16,16,2048]{2,1,0:T(8,128)(2,1)}), bf16[16,16,2048]{2,1,0:T(8,128)(2,1)}, u32[]{:S(2)}, u32[]{:S(2)}) async-start(bf16[16,16,2048]{2,1,0:T(8,128)(2,1)} %bitcast.135), calls=%async_computation.3 | async-start | bytes 2097152 | tf_op jit(solution)/shard_map/all_to_all | solution.py:189
  141.0 3.2 fusion.26
  144.2 21.3 %all-to-all-done.3 = bf16[16,16,2048]{2,1,0:T(8,128)(2,1)} async-done(((bf16[16,16,2048]{2,1,0:T(8,128)(2,1)}), bf16[16,16,2048]{2,1,0:T(8,128)(2,1)}, u32[]{:S(2)}, u32[]{:S(2)}) %all-to-all-start.3) | async-done | bytes 1048608 | tf_op jit(solution)/shard_map/all_to_all | solution.py:189
  165.5 2.5 fusion.48
  168.0 2.8 multiply_convert_fusion.2
  171.6 1.7 fusion.1
  173.3 4.8 %all-to-all-start.5 = ((bf16[16,16,2048]{2,1,0:T(8,128)(2,1)}), bf16[16,16,2048]{2,1,0:T(8,128)(2,1)}, u32[]{:S(2)}, u32[]{:S(2)}) async-start(bf16[16,16,2048]{2,1,0:T(8,128)(2,1)} %bitcast.147), calls=%async_computation.5 | async-start | bytes 2097152 | tf_op jit(solution)/shard_map/all_to_all | solution.py:189
  178.1 2.4 shard_map.116
  181.4 20.8 %all-to-all-done.5 = bf16[16,16,2048]{2,1,0:T(8,128)(2,1)} async-done(((bf16[16,16,2048]{2,1,0:T(8,128)(2,1)}), bf16[16,16,2048]{2,1,0:T(8,128)(2,1)}, u32[]{:S(2)}, u32[]{:S(2)}) %all-to-all-start.5) | async-done | bytes 1048608 | tf_op jit(solution)/shard_map/all_to_all | solution.py:189
  202.3 4.9 %all-to-all-start.7 = ((bf16[16,16,2048]{2,1,0:T(8,128)(2,1)}), bf16[16,16,2048]{2,1,0:T(8,128)(2,1)}, u32[]{:S(2)}, u32[]{:S(2)}) async-start(bf16[16,16,2048]{2,1,0:T(8,128)(2,1)} %bitcast.128), calls=%async_computation.7 | async-start | bytes 2097152 | tf_op jit(solution)/shard_map/all_to_all | solution.py:189
  207.2 1.0 copy-done.3
  208.2 1.2 copy-done.14
  209.4 5.9 %shard_map.115 = (bf16[256,2048]{1,0:T(8,128)(2,1)S(1)}, f32[128,2048]{1,0:T(8,128)S(1)}) custom-call(s32[2,128]{1,0:T(2,128)S(1)} %get-tuple-element.37.next_ids_ref.ids_ref, s32[2,128]{1,0:T(2,128)S(1)} %get-tuple-element.38.next_ids_ref.ids_ref, f32[2,128]{1,0:T(2,128)S(1)} %get-tuple-element.34.next_probs_ref, bf16[256,2048]{1,0:T(8,128)(2,1)} %bitcast.27.back_ref, ...), custom_call_target="tpu_custom_call" | custom-call | flops 402653184 | bytes 6291456 | tf_op jit(solution)/shard_map/pallas_call | solution.py:242
  217.3 14.3 %all-to-all-done.7 = bf16[16,16,2048]{2,1,0:T(8,128)(2,1)} async-done(((bf16[16,16,2048]{2,1,0:T(8,128)(2,1)}), bf16[16,16,2048]{2,1,0:T(8,128)(2,1)}, u32[]{:S(2)}, u32[]{:S(2)}) %all-to-all-start.7) | async-done | bytes 1048608 | tf_op jit(solution)/shard_map/all_to_all | solution.py:189
  231.6 4.8 %all-to-all-start.6 = ((bf16[16,16,2048]{2,1,0:T(8,128)(2,1)}), bf16[16,16,2048]{2,1,0:T(8,128)(2,1)}, u32[]{:S(2)}, u32[]{:S(2)}) async-start(bf16[16,16,2048]{2,1,0:T(8,128)(2,1)} %bitcast.134), calls=%async_computation.6 | async-start | bytes 2097152 | tf_op jit(solution)/shard_map/all_to_all | solution.py:189
  236.4 3.2 fusion.22
  239.6 21.0 %all-to-all-done.6 = bf16[16,16,2048]{2,1,0:T(8,128)(2,1)} async-done(((bf16[16,16,2048]{2,1,0:T(8,128)(2,1)}), bf16[16,16,2048]{2,1,0:T(8,128)(2,1)}, u32[]{:S(2)}, u32[]{:S(2)}) %all-to-all-start.6) | async-done | bytes 1048608 | tf_op jit(solution)/shard_map/all_to_all | solution.py:189
  260.6 2.5 fusion.46
  263.1 2.8 multiply_convert_fusion.1
  266.6 1.7 fusion.2
  268.4 5.1 %all-to-all-start.8 = ((bf16[16,16,2048]{2,1,0:T(8,128)(2,1)}), bf16[16,16,2048]{2,1,0:T(8,128)(2,1)}, u32[]{:S(2)}, u32[]{:S(2)}) async-start(bf16[16,16,2048]{2,1,0:T(8,128)(2,1)} %bitcast.145), calls=%async_computation.8 | async-start | bytes 2097152 | tf_op jit(solution)/shard_map/all_to_all | solution.py:189
  273.5 2.4 shard_map.118
  276.9 21.6 %all-to-all-done.8 = bf16[16,16,2048]{2,1,0:T(8,128)(2,1)} async-done(((bf16[16,16,2048]{2,1,0:T(8,128)(2,1)}), bf16[16,16,2048]{2,1,0:T(8,128)(2,1)}, u32[]{:S(2)}, u32[]{:S(2)}) %all-to-all-start.8) | async-done | bytes 1048608 | tf_op jit(solution)/shard_map/all_to_all | solution.py:189
  298.5 4.7 %all-to-all-start.10 = ((bf16[16,16,2048]{2,1,0:T(8,128)(2,1)}), bf16[16,16,2048]{2,1,0:T(8,128)(2,1)}, u32[]{:S(2)}, u32[]{:S(2)}) async-start(bf16[16,16,2048]{2,1,0:T(8,128)(2,1)} %bitcast.129), calls=%async_computation.10 | async-start | bytes 2097152 | tf_op jit(solution)/shard_map/all_to_all | solution.py:189
  303.2 1.2 copy-done.12
  304.4 5.9 %shard_map.117 = (bf16[256,2048]{1,0:T(8,128)(2,1)S(1)}, f32[128,2048]{1,0:T(8,128)S(1)}) custom-call(s32[2,128]{1,0:T(2,128)S(1)} %get-tuple-element.38.next_ids_ref.ids_ref, s32[2,128]{1,0:T(2,128)S(1)} %get-tuple-element.39.next_ids_ref.ids_ref, f32[2,128]{1,0:T(2,128)S(1)} %get-tuple-element.35.next_probs_ref, bf16[256,2048]{1,0:T(8,128)(2,1)} %bitcast.34.back_ref, ...), custom_call_target="tpu_custom_call" | custom-call | flops 402653184 | bytes 6291456 | tf_op jit(solution)/shard_map/pallas_call | solution.py:242
  312.3 15.1 %all-to-all-done.10 = bf16[16,16,2048]{2,1,0:T(8,128)(2,1)} async-done(((bf16[16,16,2048]{2,1,0:T(8,128)(2,1)}), bf16[16,16,2048]{2,1,0:T(8,128)(2,1)}, u32[]{:S(2)}, u32[]{:S(2)}) %all-to-all-start.10) | async-done | bytes 1048608 | tf_op jit(solution)/shard_map/all_to_all | solution.py:189
  327.4 4.9 %all-to-all-start.9 = ((bf16[16,16,2048]{2,1,0:T(8,128)(2,1)}), bf16[16,16,2048]{2,1,0:T(8,128)(2,1)}, u32[]{:S(2)}, u32[]{:S(2)}) async-start(bf16[16,16,2048]{2,1,0:T(8,128)(2,1)} %bitcast.133), calls=%async_computation.9 | async-start | bytes 2097152 | tf_op jit(solution)/shard_map/all_to_all | solution.py:189
  332.3 2.4 fusion.18
  334.7 21.9 %all-to-all-done.9 = bf16[16,16,2048]{2,1,0:T(8,128)(2,1)} async-done(((bf16[16,16,2048]{2,1,0:T(8,128)(2,1)}), bf16[16,16,2048]{2,1,0:T(8,128)(2,1)}, u32[]{:S(2)}, u32[]{:S(2)}) %all-to-all-start.9) | async-done | bytes 1048608 | tf_op jit(solution)/shard_map/all_to_all | solution.py:189
  356.7 2.5 pad_maximum_fusion.1
  359.3 2.7 fusion.44
  362.1 2.1 multiply_convert_fusion
  364.2 2.2 fusion.58
  367.2 1.7 fusion.3
  368.9 4.8 %all-to-all-start.11 = ((bf16[16,16,2048]{2,1,0:T(8,128)(2,1)}), bf16[16,16,2048]{2,1,0:T(8,128)(2,1)}, u32[]{:S(2)}, u32[]{:S(2)}) async-start(bf16[16,16,2048]{2,1,0:T(8,128)(2,1)} %bitcast.144), calls=%async_computation.11 | async-start | bytes 2097152 | tf_op jit(solution)/shard_map/all_to_all | solution.py:189
  373.8 2.5 pad_maximum_fusion
  376.4 2.2 fusion.55
  378.7 2.2 fusion.52
  381.3 4.6 %add_bitcast_fusion = f32[1,1024,384]{2,1,0:T(8,128)} fusion(bf16[1024,384]{1,0:T(8,128)(2,1)} %collective-permute-done.2, bf16[256,384]{1,0:T(8,128)(2,1)} %copy-done.55, bf16[256,384]{1,0:T(8,128)(2,1)} %get-tuple-element.26, bf16[256,384]{1,0:T(8,128)(2,1)} %get-tuple-element.23, bf16[256,384]{1,0:T(8,128)(2,1)} %get-tuple-element.20, ...), kind=kOutput, calls=%fused_computation.58 | convolution fusion | flops 809238528 | bytes 5242884 | tf_op jit(solution)/shard_map/dot_general | solution.py:21
  385.9 3.7 add_bitcast_fusion.1
  389.6 3.6 add_bitcast_fusion.2
  393.2 6.9 %all-to-all-done.11 = bf16[16,16,2048]{2,1,0:T(8,128)(2,1)} async-done(((bf16[16,16,2048]{2,1,0:T(8,128)(2,1)}), bf16[16,16,2048]{2,1,0:T(8,128)(2,1)}, u32[]{:S(2)}, u32[]{:S(2)}) %all-to-all-start.11) | async-done | bytes 1048608 | tf_op jit(solution)/shard_map/all_to_all | solution.py:189
  400.1 1.2 copy-done.19
  401.3 4.8 %shard_map.119 = f32[128,2048]{1,0:T(8,128)} custom-call(s32[2,128]{1,0:T(2,128)S(1)} %get-tuple-element.39.next_ids_ref.ids_ref, s32[2,128]{1,0:T(2,128)S(1)} %get-tuple-element.39.next_ids_ref.ids_ref, f32[2,128]{1,0:T(2,128)S(1)} %get-tuple-element.35.next_probs_ref, bf16[256,2048]{1,0:T(8,128)(2,1)} %bitcast.41.back_ref, ...), custom_call_target="tpu_custom_call" | custom-call | flops 402653184 | bytes 6291456 | tf_op jit(solution)/shard_map/pallas_call | solution.py:242
  (118 shorter events, 16.1 us)
Async XLA Ops:
  0.6 71.9 %copy-start = (bf16[1,2048,384]{2,1,0:T(8,128)(2,1)S(1)}, bf16[1,2048,384]{2,1,0:T(8,128)(2,1)}, u32[]{:S(2)}) copy-start(bf16[1,2048,384]{2,1,0:T(8,128)(2,1)} %param.14) | copy-start | bytes 4718596
  1.5 2.6 copy-start.20
  4.1 11.4 %copy-start.51 = (f32[4,128,2]{1,2,0:T(2,128)S(1)}, f32[4,128,2]{1,2,0:T(2,128)}, u32[]{:S(2)}) copy-start(f32[4,128,2]{1,2,0:T(2,128)} %param.10) | copy-start | bytes 12292
  4.1 11.4 %copy-start.1 = (bf16[128,2048]{1,0:T(8,128)(2,1)S(1)}, bf16[128,2048]{1,0:T(8,128)(2,1)}, u32[]{:S(2)}) copy-start(bf16[128,2048]{1,0:T(8,128)(2,1)} %end_ref.9) | copy-start | bytes 1572868
  7.3 1.0 copy-start.9
  8.2 32.9 %all-to-all-start.1 = ((bf16[16,16,2048]{2,1,0:T(8,128)(2,1)}), bf16[16,16,2048]{2,1,0:T(8,128)(2,1)}, u32[]{:S(2)}, u32[]{:S(2)}) async-start(bf16[16,16,2048]{2,1,0:T(8,128)(2,1)} %bitcast.131), calls=%async_computation.1 | async-start | bytes 2097152 | tf_op jit(solution)/shard_map/all_to_all | solution.py:189
  17.7 1.0 copy-start.10
  41.1 29.0 %all-to-all-start = ((bf16[16,16,2048]{2,1,0:T(8,128)(2,1)}), bf16[16,16,2048]{2,1,0:T(8,128)(2,1)}, u32[]{:S(2)}, u32[]{:S(2)}) async-start(bf16[16,16,2048]{2,1,0:T(8,128)(2,1)} %bitcast.132), calls=%async_computation | async-start | bytes 2097152 | tf_op jit(solution)/shard_map/all_to_all | solution.py:189
  70.0 2.5 copy-start.29
  72.6 2.8 copy-start.21
  77.9 29.3 %all-to-all-start.2 = ((bf16[16,16,2048]{2,1,0:T(8,128)(2,1)}), bf16[16,16,2048]{2,1,0:T(8,128)(2,1)}, u32[]{:S(2)}, u32[]{:S(2)}) async-start(bf16[16,16,2048]{2,1,0:T(8,128)(2,1)} %bitcast.146), calls=%async_computation.2 | async-start | bytes 2097152 | tf_op jit(solution)/shard_map/all_to_all | solution.py:189
  82.8 1.0 copy-start.2
  86.2 1.0 copy-start.8
  107.2 28.9 %all-to-all-start.4 = ((bf16[16,16,2048]{2,1,0:T(8,128)(2,1)}), bf16[16,16,2048]{2,1,0:T(8,128)(2,1)}, u32[]{:S(2)}, u32[]{:S(2)}) async-start(bf16[16,16,2048]{2,1,0:T(8,128)(2,1)} %bitcast.130), calls=%async_computation.4 | async-start | bytes 2097152 | tf_op jit(solution)/shard_map/all_to_all | solution.py:189
  112.0 1.0 copy-start.5
  118.9 1.0 copy-start.13
  119.9 1.0 copy-start.17
  136.1 29.4 %all-to-all-start.3 = ((bf16[16,16,2048]{2,1,0:T(8,128)(2,1)}), bf16[16,16,2048]{2,1,0:T(8,128)(2,1)}, u32[]{:S(2)}, u32[]{:S(2)}) async-start(bf16[16,16,2048]{2,1,0:T(8,128)(2,1)} %bitcast.135), calls=%async_computation.3 | async-start | bytes 2097152 | tf_op jit(solution)/shard_map/all_to_all | solution.py:189
  165.5 2.5 copy-start.30
  168.0 2.8 copy-start.22
  173.3 29.0 %all-to-all-start.5 = ((bf16[16,16,2048]{2,1,0:T(8,128)(2,1)}), bf16[16,16,2048]{2,1,0:T(8,128)(2,1)}, u32[]{:S(2)}, u32[]{:S(2)}) async-start(bf16[16,16,2048]{2,1,0:T(8,128)(2,1)} %bitcast.147), calls=%async_computation.5 | async-start | bytes 2097152 | tf_op jit(solution)/shard_map/all_to_all | solution.py:189
  180.5 1.0 copy-start.6
  202.3 29.3 %all-to-all-start.7 = ((bf16[16,16,2048]{2,1,0:T(8,128)(2,1)}), bf16[16,16,2048]{2,1,0:T(8,128)(2,1)}, u32[]{:S(2)}, u32[]{:S(2)}) async-start(bf16[16,16,2048]{2,1,0:T(8,128)(2,1)} %bitcast.128), calls=%async_computation.7 | async-start | bytes 2097152 | tf_op jit(solution)/shard_map/all_to_all | solution.py:189
  207.2 1.0 copy-start.3
  208.2 1.2 copy-start.14
  215.4 1.0 copy-start.11
  231.6 28.9 %all-to-all-start.6 = ((bf16[16,16,2048]{2,1,0:T(8,128)(2,1)}), bf16[16,16,2048]{2,1,0:T(8,128)(2,1)}, u32[]{:S(2)}, u32[]{:S(2)}) async-start(bf16[16,16,2048]{2,1,0:T(8,128)(2,1)} %bitcast.134), calls=%async_computation.6 | async-start | bytes 2097152 | tf_op jit(solution)/shard_map/all_to_all | solution.py:189
  260.6 2.5 copy-start.31
  263.0 2.8 copy-start.23
  268.4 30.1 %all-to-all-start.8 = ((bf16[16,16,2048]{2,1,0:T(8,128)(2,1)}), bf16[16,16,2048]{2,1,0:T(8,128)(2,1)}, u32[]{:S(2)}, u32[]{:S(2)}) async-start(bf16[16,16,2048]{2,1,0:T(8,128)(2,1)} %bitcast.145), calls=%async_computation.8 | async-start | bytes 2097152 | tf_op jit(solution)/shard_map/all_to_all | solution.py:189
  275.9 1.0 copy-start.7
  298.5 29.0 %all-to-all-start.10 = ((bf16[16,16,2048]{2,1,0:T(8,128)(2,1)}), bf16[16,16,2048]{2,1,0:T(8,128)(2,1)}, u32[]{:S(2)}, u32[]{:S(2)}) async-start(bf16[16,16,2048]{2,1,0:T(8,128)(2,1)} %bitcast.129), calls=%async_computation.10 | async-start | bytes 2097152 | tf_op jit(solution)/shard_map/all_to_all | solution.py:189
  303.2 1.2 copy-start.12
  310.4 1.0 copy-start.15
  311.3 1.0 copy-start.18
  327.4 29.3 %all-to-all-start.9 = ((bf16[16,16,2048]{2,1,0:T(8,128)(2,1)}), bf16[16,16,2048]{2,1,0:T(8,128)(2,1)}, u32[]{:S(2)}, u32[]{:S(2)}) async-start(bf16[16,16,2048]{2,1,0:T(8,128)(2,1)} %bitcast.133), calls=%async_computation.9 | async-start | bytes 2097152 | tf_op jit(solution)/shard_map/all_to_all | solution.py:189
  356.7 2.7 copy-start.25
  359.3 4.8 %copy-start.26 = (bf16[1024,2048]{1,0:T(8,128)(2,1)}, bf16[1024,2048]{1,0:T(8,128)(2,1)S(1)}, u32[]{:S(2)}) copy-start(bf16[1024,2048]{1,0:T(8,128)(2,1)S(1)} %pad_maximum_fusion.1) | copy-start | bytes 12582916
  362.0 2.2 copy-start.52
  362.0 2.2 copy-start.53
  362.0 2.2 copy-start.54
  364.1 2.3 copy-start.55
  364.2 2.3 copy-start.48
  364.2 3.0 copy-start.36
  364.2 2.2 copy-start.24
  366.4 14.9 %collective-permute-start.2 = (bf16[1024,384]{1,0:T(8,128)(2,1)}, bf16[1024,384]{1,0:T(8,128)(2,1)}, u32[]{:S(2)}, u32[]{:S(2)}) collective-permute-start(bf16[1024,384]{1,0:T(8,128)(2,1)} %fusion.58), channel_id=1, source_target_pairs={{0,16},{16,0},{1,17},{17,1},{2,18},{18,2},{3,19},{19,3},{4,20},{20... | collective-permute-start | bytes 2359304 | tf_op jit(solution)/shard_map/ppermute | solution.py:276
  368.9 31.1 %all-to-all-start.11 = ((bf16[16,16,2048]{2,1,0:T(8,128)(2,1)}), bf16[16,16,2048]{2,1,0:T(8,128)(2,1)}, u32[]{:S(2)}, u32[]{:S(2)}) async-start(bf16[16,16,2048]{2,1,0:T(8,128)(2,1)} %bitcast.144), calls=%async_computation.11 | async-start | bytes 2097152 | tf_op jit(solution)/shard_map/all_to_all | solution.py:189
  373.8 2.5 copy-start.33
  373.8 2.5 copy-start.35
  373.8 2.5 copy-start.37
  376.3 2.4 copy-start.27
  376.3 2.4 copy-start.40
  376.3 2.4 copy-start.43
  376.3 2.4 copy-start.46
  376.3 2.4 copy-start.49
  378.6 7.4 %collective-permute-start.1 = (bf16[1024,384]{1,0:T(8,128)(2,1)}, bf16[1024,384]{1,0:T(8,128)(2,1)}, u32[]{:S(2)}, u32[]{:S(2)}) collective-permute-start(bf16[1024,384]{1,0:T(8,128)(2,1)} %fusion.55), channel_id=1, source_target_pairs={{0,16},{16,0},{1,17},{17,1},{2,18},{18,2},{3,19},{19,3},{4,20},{20... | collective-permute-start | bytes 2359304 | tf_op jit(solution)/shard_map/ppermute | solution.py:276
  380.9 8.7 %collective-permute-start = (bf16[1024,384]{1,0:T(8,128)(2,1)}, bf16[1024,384]{1,0:T(8,128)(2,1)}, u32[]{:S(2)}, u32[]{:S(2)}) collective-permute-start(bf16[1024,384]{1,0:T(8,128)(2,1)} %fusion.52), channel_id=1, source_target_pairs={{0,16},{16,0},{1,17},{17,1},{2,18},{18,2},{3,19},{19,3},{4,20},{20... | collective-permute-start | bytes 2359304 | tf_op jit(solution)/shard_map/ppermute | solution.py:276
  381.3 4.6 %copy-start.28 = (bf16[1024,2048]{1,0:T(8,128)(2,1)S(1)}, bf16[1024,2048]{1,0:T(8,128)(2,1)}, u32[]{:S(2)}) copy-start(bf16[1024,2048]{1,0:T(8,128)(2,1)} %copy-done.27) | copy-start | bytes 12582916
  381.3 4.6 %copy-start.38 = (bf16[256,384]{1,0:T(8,128)(2,1)S(1)}, bf16[256,384]{1,0:T(8,128)(2,1)}, u32[]{:S(2)}) copy-start(bf16[256,384]{1,0:T(8,128)(2,1)} %copy-done.36) | copy-start | bytes 589828
  385.9 3.7 copy-start.41
  385.9 3.7 copy-start.44
  385.9 3.7 copy-start.47
  385.9 3.7 copy-start.50
  400.1 1.2 copy-start.19
  (7 other events, 5.5 us)
